TPU v7x, 32 devices: a whole 2x2x4 slice. The times are simulated.
32 devices in a mesh: layer: 4 (over y, x), row: 2 (over core), col: 4 (over z).
Axes of the slice: x: 2, y: 2, z: 4, core: 2. Of those that a mesh axis runs over, the one named last changes fastest.
Arguments:
- hidden: bfloat16 [384, 2304], P(('layer', 'row')), may hold values from -60 to 60
- embedding: bfloat16 [16384, 2304], P(('row', 'col'), 'layer'), may hold values from -0.3 to 0.3
- teacher: bfloat16 [384, 16384], P('layer', ('row', 'col')), may hold values from -80 to 240
Outputs:
- grad_embedding: float32 [16384, 2304], P(('row', 'col'), 'layer')
- grad_hidden: float32 [384, 2304], P(('layer', 'row', 'col'))
All inputs are finite; a program needn't handle non-finite values.
Results may differ from a plain program's by a relative error of at most 0.0041.
Values may be sent and summed in bfloat16 or wider, within the bound.
A program may use at most 192 MiB of HBM per device.

v0:
```python
import jax
import jax.numpy as jnp
from jax import lax
from jax.sharding import PartitionSpec as P

LOSS_SCALE = 256


def local(hidden, embedding, teacher):
    token_rows = lax.all_gather(hidden, "row", axis=0, tiled=True)
    width_part = lax.all_to_all(token_rows, "layer", split_axis=1, concat_axis=0, tiled=True)
    logits = lax.psum_scatter(
        lax.dot_general(
            width_part, embedding, (((1,), (1,)), ((), ())), preferred_element_type=jnp.float32
        ),
        "layer",
        scatter_dimension=0,
        tiled=True,
    )
    teach_f = teacher.astype(jnp.float32)
    top_s, top_t = lax.pmax((jnp.max(logits, axis=1), jnp.max(teach_f, axis=1)), ("row", "col"))
    part_s = jnp.sum(jnp.exp(logits - top_s[:, None]), axis=1)
    part_t = jnp.sum(jnp.exp(teach_f - top_t[:, None]), axis=1)
    sum_s, sum_t = lax.psum((part_s, part_t), ("row", "col"))
    lse_s = top_s + jnp.log(sum_s)
    lse_t = top_t + jnp.log(sum_t)
    prob_s = jnp.exp(logits - lse_s[:, None])
    prob_t = jnp.exp(teach_f - lse_t[:, None])
    grads = ((prob_s - prob_t) * LOSS_SCALE).astype(jnp.bfloat16)
    grad_piece = lax.all_gather(grads, "layer", axis=0, tiled=True)
    embed_acc = lax.dot_general(
        grad_piece, width_part, (((0,), (0,)), ((), ())), preferred_element_type=jnp.float32
    )
    hidden_piece = jnp.dot(grad_piece, embedding, preferred_element_type=jnp.float32)
    hidden_terms = lax.all_to_all(hidden_piece, "layer", split_axis=0, concat_axis=1, tiled=True)
    grad_hidden = lax.psum_scatter(hidden_terms, ("row", "col"), scatter_dimension=0, tiled=True)
    return (embed_acc, grad_hidden)


def solution(mesh):
    placed = (P(("layer", "row"), None), P(("row", "col"), "layer"), P("layer", ("row", "col")))
    return jax.shard_map(
        local,
        mesh=mesh,
        in_specs=placed,
        out_specs=(P(("row", "col"), "layer"), P(("layer", "row", "col"), None)),
        check_vma=False,
    )
```

profile of v0, /device:TPU:1, one launch (start us, length us, event | category | flops | bytes accessed | tf_op | source)
XLA Modules:
  0.0 216.0 jit_solution(10763876937868347929)
XLA Ops:
  7.2 0.0 copy-start
  7.2 0.0 reduce-scatter.4.cloned.1.call-start
  7.2 2.5 %all_gather.6 = bf16[96,2304]{1,0:T(8,128)(2,1)S(1)} all-gather(bf16[48,2304]{1,0:T(8,128)(2,1)} %param.3), channel_id=1, replica_groups=mesh['layer'=4,'row'=2,'col'=4] {'row'}, dimensions={0}, use_global_device_ids=true | all-gather | bytes 663552 | tf_op jit(solution)/shard_map/all_gather | solution.py:10
  9.7 0.6 all_to_all.28
  10.3 0.1 copy.11
  10.3 11.5 %all_to_all.38 = bf16[96,4,576]{2,0,1:T(8,128)(2,1)S(1)} all-to-all(bf16[96,4,576]{2,0,1:T(8,128)(2,1)S(1)} %copy.11), channel_id=1, replica_groups=mesh['layer'=4,'row'=2,'col'=4] {'layer'}, dimensions={1} | all-to-all | bytes 884736 | tf_op jit(solution)/shard_map/all_to_all | solution.py:11
  21.8 0.0 copy-start.2
  21.8 0.8 copy-done.2
  22.6 0.0 copy-done
  22.6 3.1 %fusion.7 = f32[384,2048]{1,0:T(8,128)} fusion(bf16[384,576]{1,0:T(8,128)(2,1)S(1)} %bitcast.14, bf16[2048,576]{0,1:T(8,128)(2,1)S(1)} %copy-done), kind=kOutput, calls=%fused_computation.12 | convolution fusion | flops 905969664 | bytes 5947392 | tf_op jit(solution)/shard_map/dot_general | solution.py:13
  25.7 0.0 copy-start.5
  25.7 0.0 reduce-scatter.4.cloned.1.call-update
  25.7 0.0 all-gather.2.cloned.1.call-start
  25.8 0.9 copy-done.5
  26.7 0.2 reduce_max.24
  26.8 43.8 %reduce-scatter.4.cloned.1.call-done = f32[96,2048]{1,0:T(8,128)} async-done(((f32[384,2048]{1,0:T(8,128)}), f32[96,2048]{1,0:T(8,128)}) %reduce-scatter.4.cloned.1.call-update) | async-done | bytes 786448 | tf_op jit(solution)/shard_map/reduce_scatter | solution.py:12
  70.6 0.0 copy-start.1
  70.6 1.3 reduce_max.23
  72.0 17.8 %all-reduce.3 = (f32[96]{0:T(128)S(1)}, f32[96]{0:T(128)S(1)}) all-reduce(bf16[96]{0:T(256)(128)(2,1)S(1)} %reduce_max.24, f32[96]{0:T(128)S(1)} %reduce_max.23), channel_id=1, replica_groups=mesh['layer'=4,'row'=2,'col'=4] {'row','col'}, use_global_device_ids=true, to_apply=%region_6.0 | all-reduce | flops 192 | bytes 1344 | tf_op jit(solution)/shard_map/pmax | solution.py:21
  89.8 1.5 fusion.2
  91.4 14.2 %all-reduce.2 = (f32[96]{0:T(128)}, f32[96]{0:T(128)}) all-reduce(f32[96]{0:T(128)S(1)} %get-tuple-element.6, f32[96]{0:T(128)S(1)} %get-tuple-element.7), channel_id=1, replica_groups=mesh['layer'=4,'row'=2,'col'=4] {'row','col'}, use_global_device_ids=true, to_apply=%region_8.0 | all-reduce | flops 192 | bytes 1536 | tf_op jit(solution)/shard_map/psum | solution.py:24
  105.6 0.7 log_add_fusion
  106.2 0.7 log_add_fusion.1
  106.9 0.0 copy-done.1
  106.9 1.1 fusion.6
  108.0 0.0 all-gather.2.cloned.1.call-update
  108.0 0.0 copy-start.6
  108.0 29.8 %all-gather.2.cloned.1.call-done = bf16[384,2048]{1,0:T(8,128)(2,1)} async-done(((bf16[96,2048]{1,0:T(8,128)(2,1)}), bf16[384,2048]{1,0:T(8,128)(2,1)}) %all-gather.2.cloned.1.call-update) | async-done | bytes 1572880 | tf_op jit(solution)/shard_map/all_gather | solution.py:30
  137.8 3.8 %fusion.9 = f32[384,576]{1,0:T(8,128)} fusion(bf16[384,2048]{1,0:T(8,128)(2,1)} %all-gather.2.cloned.1.call-done, bf16[2048,576]{0,1:T(8,128)(2,1)S(1)} %copy-done), kind=kOutput, calls=%fused_computation.14 | convolution fusion | flops 905969664 | bytes 4816896 | tf_op jit(solution)/shard_map/dot_general | solution.py:34
  141.6 3.5 %all-to-all-start.1 = ((f32[4,96,576]{2,1,0:T(8,128)}), f32[4,96,576]{2,1,0:T(8,128)S(1)}, u32[]{:S(2)}, u32[]{:S(2)}) async-start(f32[4,96,576]{2,1,0:T(8,128)} %bitcast.17), calls=%async_computation.2 | async-start | bytes 1966080 | tf_op jit(solution)/shard_map/all_to_all | solution.py:35
  145.1 0.0 copy-done.6
  145.1 0.6 dynamic-slice.4
  146.3 11.2 %all-to-all-done.1 = f32[4,96,576]{2,1,0:T(8,128)S(1)} async-done(((f32[4,96,576]{2,1,0:T(8,128)}), f32[4,96,576]{2,1,0:T(8,128)S(1)}, u32[]{:S(2)}, u32[]{:S(2)}) %all-to-all-start.1) | async-done | bytes 884768 | tf_op jit(solution)/shard_map/all_to_all | solution.py:35
  157.5 0.0 copy-start.4
  157.5 0.9 copy-done.4
  158.4 0.0 copy-start.3
  158.4 2.8 %copy.13 = f32[96,4,576]{2,1,0:T(4,128)} copy(f32[96,4,576]{2,0,1:T(8,128)} %bitcast.16) | data formatting | bytes 1769472 | tf_op jit(solution)/shard_map/all_to_all | solution.py:35
  161.3 2.7 %all_to_all.35 = f32[96,2304]{1,0:T(8,128)} reshape(f32[96,4,576]{2,1,0:T(4,128)} %copy.13) | data formatting | bytes 1769472 | tf_op jit(solution)/shard_map/all_to_all | solution.py:35
  164.0 32.7 %fusion = f32[16,2304]{1,0:T(8,128)S(1)} fusion(f32[96,2304]{1,0:T(8,128)} %all_to_all.35), kind=kCustom, calls=%all-reduce-scatter | all-reduce-scatter fusion | flops 294913 | bytes 1032704
  196.7 1.9 collective-permute-start
  198.6 2.4 %collective-permute-start.1 = (f32[12,2304]{1,0:T(8,128)S(1)}, f32[12,2304]{1,0:T(8,128)S(1)}, u32[]{:S(2)}, u32[]{:S(2)}) collective-permute-start(f32[12,2304]{1,0:T(8,128)S(1)} %slice), channel_id=1, source_target_pairs={{0,2},{1,3},{2,4},{3,5},{4,6},{5,7},{8,10},{9,11},{10,12},{11,13},... | collective-permute-start | bytes 331784
  201.0 0.0 copy-done.3
  201.0 5.0 %fusion.8 = f32[2048,576]{0,1:T(8,128)} fusion(bf16[384,2048]{1,0:T(8,128)(2,1)} %all-gather.2.cloned.1.call-done, bf16[384,576]{1,0:T(8,128)(2,1)S(1)} %bitcast.15), kind=kOutput, calls=%fused_computation.13 | convolution fusion | flops 905969664 | bytes 6733824 | tf_op jit(solution)/shard_map/dot_general | solution.py:31
  206.1 2.0 collective-permute-done.1
  208.1 0.0 collective-permute-done
  208.1 0.4 concatenate
  208.5 0.7 constant_dynamic-slice_fusion
  (1 shorter events, 0.0 us)
Async XLA Ops:
  7.2 15.5 %copy-start = (bf16[2048,576]{0,1:T(8,128)(2,1)S(1)}, bf16[2048,576]{0,1:T(8,128)(2,1)}, u32[]{:S(2)}) copy-start(bf16[2048,576]{0,1:T(8,128)(2,1)} %param.4) | copy-start | bytes 7077892
  7.2 63.5 %reduce-scatter.4.cloned.1.call-start = ((), (), s32[]{:S(2)}) async-start(), calls=%async_computation.3 | async-start | bytes 3932160 | tf_op jit(solution)/shard_map/reduce_scatter | solution.py:12
  21.8 0.8 copy-start.2
  25.7 1.0 copy-start.5
  25.7 112.1 %all-gather.2.cloned.1.call-start = ((), (), s32[]{:S(2)}) async-start(), calls=%async_computation.4 | async-start | bytes 1966080 | tf_op jit(solution)/shard_map/all_gather | solution.py:30
  70.6 36.2 %copy-start.1 = (f32[96,2048]{1,0:T(8,128)S(1)}, f32[96,2048]{1,0:T(8,128)}, u32[]{:S(2)}) copy-start(f32[96,2048]{1,0:T(8,128)} %reduce-scatter.4.cloned.1.call-done) | copy-start | bytes 2359300
  108.0 37.1 %copy-start.6 = (u32[32]{0:T(128)S(1)}, u32[32]{0:T(128)}, u32[]{:S(2)}) copy-start(u32[32]{0:T(128)} %constant.10) | copy-start | bytes 388
  141.6 15.9 %all-to-all-start.1 = ((f32[4,96,576]{2,1,0:T(8,128)}), f32[4,96,576]{2,1,0:T(8,128)S(1)}, u32[]{:S(2)}, u32[]{:S(2)}) async-start(f32[4,96,576]{2,1,0:T(8,128)} %bitcast.17), calls=%async_computation.2 | async-start | bytes 1966080 | tf_op jit(solution)/shard_map/all_to_all | solution.py:35
  157.5 0.9 copy-start.4
  158.4 42.6 %copy-start.3 = (bf16[96,4,576]{2,0,1:T(8,128)(2,1)S(1)}, bf16[96,4,576]{2,0,1:T(8,128)(2,1)}, u32[]{:S(2)}) copy-start(bf16[96,4,576]{2,0,1:T(8,128)(2,1)} %copy-done.2) | copy-start | bytes 1327108
  196.7 11.4 %collective-permute-start = (f32[16,2304]{1,0:T(8,128)S(1)}, f32[16,2304]{1,0:T(8,128)S(1)}, u32[]{:S(2)}, u32[]{:S(2)}) collective-permute-start(f32[16,2304]{1,0:T(8,128)S(1)} %fusion), channel_id=1, source_target_pairs={{0,1},{1,2},{2,3},{3,4},{4,5},{5,6},{6,7},{8,9},{9,10},{10,11},{11... | collective-permute-start | bytes 442376
  198.6 9.5 %collective-permute-start.1 = (f32[12,2304]{1,0:T(8,128)S(1)}, f32[12,2304]{1,0:T(8,128)S(1)}, u32[]{:S(2)}, u32[]{:S(2)}) collective-permute-start(f32[12,2304]{1,0:T(8,128)S(1)} %slice), channel_id=1, source_target_pairs={{0,2},{1,3},{2,4},{3,5},{4,6},{5,7},{8,10},{9,11},{10,12},{11,13},... | collective-permute-start | bytes 331784
Sparse Core Ops, SparseCore 0:
  25.8 44.7 reduce-scatter.3
  108.1 29.6 all-gather.1
where the time goes:
time: 217 us; the launch traced here: 216 us
  waiting for transfers between devices  86.8 us (40%)
  blocking collectives  78.7 us (36%)
  between operations  14.8 us (7%)
  matrix products  11.9 us (5%)
  local copies, waits for them, and re-layouts  10.5 us (5%)
  starting transfers between devices  7.91 us (4%)
  other arithmetic  5.41 us (2%)
    reduce_scatter x1, waiting for transfers between devices, local(): lax.psum_scatter(lax.dot_general(width_part, embedding, (((1,), (1,)), ((...  43.8 us
    unnamed x1, blocking collectives  32.7 us
    all_gather x1, waiting for transfers between devices, local(): grad_piece = lax.all_gather(grads, 'layer', axis=0, tiled=True)  29.8 us
    pmax x1, blocking collectives, local(): lax.pmax((jnp.max(logits, axis=1), jnp.max(teach_f, axis=1)), ('row', 'co...  17.8 us
    psum x1, blocking collectives, local(): sum_s, sum_t = lax.psum((part_s, part_t), ('row', 'col'))  14.2 us
    all_to_all x1, blocking collectives, local(): lax.all_to_all(token_rows, 'layer', split_axis=1, concat_axis=0, tiled=True)  11.5 us
    all_to_all x1, waiting for transfers between devices, local(): lax.all_to_all(hidden_piece, 'layer', split_axis=0, concat_axis=1, tiled=...  11.2 us
    all_to_all x2, local copies, waits for them, and re-layouts, local(): lax.all_to_all(hidden_piece, 'layer', split_axis=0, concat_axis=1, tiled=...  5.53 us
  transfers between devices with their start and end apart: 5, of which 4 were waited for; matrix products, arithmetic and copies ran while one was open for 3% of the time, Pallas kernels for 0%

commit v1 on v0

--- a/solution.py
+++ b/solution.py
@@ -21,7 +21,7 @@
     top_s, top_t = lax.pmax((jnp.max(logits, axis=1), jnp.max(teach_f, axis=1)), ("row", "col"))
     part_s = jnp.sum(jnp.exp(logits - top_s[:, None]), axis=1)
     part_t = jnp.sum(jnp.exp(teach_f - top_t[:, None]), axis=1)
-    sum_s, sum_t = lax.psum((part_s, part_t), ("row", "col"))
+    sum_s, sum_t = lax.psum(lax.psum((part_s, part_t), "row"), "col")
     lse_s = top_s + jnp.log(sum_s)
     lse_t = top_t + jnp.log(sum_t)
     prob_s = jnp.exp(logits - lse_s[:, None])

time: 217 us -> 212 us (0.977)
  blocking collectives: 78.7 us -> 74.2 us
    psum x1 -> x2, blocking collectives: 14.2 us -> 9.72 us  [local(): sum_s, sum_t = lax.psum(lax.psum((part_s, part_t), 'row'), 'col')]
where the time goes in v1:
time: 212 us; the launch traced here: 211 us
  waiting for transfers between devices  87.8 us (41%)
  blocking collectives  74.2 us (35%)
  between operations  14.8 us (7%)
  matrix products  11.9 us (6%)
  local copies, waits for them, and re-layouts  10.5 us (5%)
  starting transfers between devices  7.91 us (4%)
  other arithmetic  4.11 us (2%)
    reduce_scatter x1, waiting for transfers between devices, local(): lax.psum_scatter(lax.dot_general(width_part, embedding, (((1,), (1,)), ((...  43.8 us
    unnamed x1, blocking collectives  32.7 us
    all_gather x1, waiting for transfers between devices, local(): grad_piece = lax.all_gather(grads, 'layer', axis=0, tiled=True)  30.7 us
    pmax x1, blocking collectives, local(): lax.pmax((jnp.max(logits, axis=1), jnp.max(teach_f, axis=1)), ('row', 'co...  17.8 us
    all_to_all x1, blocking collectives, local(): lax.all_to_all(token_rows, 'layer', split_axis=1, concat_axis=0, tiled=True)  11.5 us
    all_to_all x1, waiting for transfers between devices, local(): lax.all_to_all(hidden_piece, 'layer', split_axis=0, concat_axis=1, tiled=...  11.2 us
    psum x2, blocking collectives, local(): sum_s, sum_t = lax.psum(lax.psum((part_s, part_t), 'row'), 'col')  9.72 us
    all_to_all x2, local copies, waits for them, and re-layouts, local(): lax.all_to_all(hidden_piece, 'layer', split_axis=0, concat_axis=1, tiled=...  5.53 us
  transfers between devices with their start and end apart: 5, of which 4 were waited for; matrix products, arithmetic and copies ran while one was open for 3% of the time, Pallas kernels for 0%

profile of v1, /device:TPU:1, one launch (start us, length us, event | category | flops | bytes accessed | tf_op | source)
XLA Modules:
  0.0 211.2 jit_solution(16825803821972433941)
XLA Ops:
  7.2 0.0 copy-start
  7.2 0.0 reduce-scatter.4.cloned.1.call-start
  7.2 2.5 %all_gather.6 = bf16[96,2304]{1,0:T(8,128)(2,1)S(1)} all-gather(bf16[48,2304]{1,0:T(8,128)(2,1)} %param.3), channel_id=1, replica_groups=mesh['layer'=4,'row'=2,'col'=4] {'row'}, dimensions={0}, use_global_device_ids=true | all-gather | bytes 663552 | tf_op jit(solution)/shard_map/all_gather | solution.py:10
  9.7 0.6 all_to_all.28
  10.3 0.1 copy.11
  10.3 11.5 %all_to_all.38 = bf16[96,4,576]{2,0,1:T(8,128)(2,1)S(1)} all-to-all(bf16[96,4,576]{2,0,1:T(8,128)(2,1)S(1)} %copy.11), channel_id=1, replica_groups=mesh['layer'=4,'row'=2,'col'=4] {'layer'}, dimensions={1} | all-to-all | bytes 884736 | tf_op jit(solution)/shard_map/all_to_all | solution.py:11
  21.8 0.0 copy-start.2
  21.8 0.8 copy-done.2
  22.6 0.0 copy-done
  22.6 3.1 %fusion.7 = f32[384,2048]{1,0:T(8,128)} fusion(bf16[384,576]{1,0:T(8,128)(2,1)S(1)} %bitcast.14, bf16[2048,576]{0,1:T(8,128)(2,1)S(1)} %copy-done), kind=kOutput, calls=%fused_computation.12 | convolution fusion | flops 905969664 | bytes 5947392 | tf_op jit(solution)/shard_map/dot_general | solution.py:13
  25.7 0.0 copy-start.5
  25.7 0.0 reduce-scatter.4.cloned.1.call-update
  25.7 0.0 all-gather.2.cloned.1.call-start
  25.8 0.9 copy-done.5
  26.7 0.2 reduce_max.24
  26.8 43.8 %reduce-scatter.4.cloned.1.call-done = f32[96,2048]{1,0:T(8,128)} async-done(((f32[384,2048]{1,0:T(8,128)}), f32[96,2048]{1,0:T(8,128)}) %reduce-scatter.4.cloned.1.call-update) | async-done | bytes 786448 | tf_op jit(solution)/shard_map/reduce_scatter | solution.py:12
  70.6 0.0 copy-start.1
  70.6 1.3 reduce_max.23
  72.0 17.8 %all-reduce.2 = (f32[96]{0:T(128)S(1)}, f32[96]{0:T(128)S(1)}) all-reduce(bf16[96]{0:T(256)(128)(2,1)S(1)} %reduce_max.24, f32[96]{0:T(128)S(1)} %reduce_max.23), channel_id=1, replica_groups=mesh['layer'=4,'row'=2,'col'=4] {'row','col'}, use_global_device_ids=true, to_apply=%region_7.0 | all-reduce | flops 192 | bytes 1344 | tf_op jit(solution)/shard_map/pmax | solution.py:21
  89.8 1.5 fusion.2
  91.4 3.0 %all-reduce.4 = (f32[96]{0:T(128)}, f32[96]{0:T(128)}) all-reduce(f32[96]{0:T(128)S(1)} %get-tuple-element.8, f32[96]{0:T(128)S(1)} %get-tuple-element.9), channel_id=1, replica_groups=mesh['layer'=4,'row'=2,'col'=4] {'row'}, use_global_device_ids=true, to_apply=%region_9.0 | all-reduce | flops 192 | bytes 1536 | tf_op jit(solution)/shard_map/psum | solution.py:24
  94.3 6.7 %all-reduce.3 = (f32[96]{0:T(128)S(1)}, f32[96]{0:T(128)S(1)}) all-reduce(f32[96]{0:T(128)} %get-tuple-element.6, f32[96]{0:T(128)} %get-tuple-element.7), channel_id=1, replica_groups=mesh['layer'=4,'row'=2,'col'=4] {'col'}, use_global_device_ids=true, to_apply=%region_10.0 | all-reduce | flops 192 | bytes 1536 | tf_op jit(solution)/shard_map/psum | solution.py:24
  101.1 0.0 copy-done.1
  101.1 1.1 fusion.6
  102.2 0.0 all-gather.2.cloned.1.call-update
  102.2 0.0 copy-start.6
  102.2 30.7 %all-gather.2.cloned.1.call-done = bf16[384,2048]{1,0:T(8,128)(2,1)} async-done(((bf16[96,2048]{1,0:T(8,128)(2,1)}), bf16[384,2048]{1,0:T(8,128)(2,1)}) %all-gather.2.cloned.1.call-update) | async-done | bytes 1572880 | tf_op jit(solution)/shard_map/all_gather | solution.py:30
  132.9 3.8 %fusion.9 = f32[384,576]{1,0:T(8,128)} fusion(bf16[384,2048]{1,0:T(8,128)(2,1)} %all-gather.2.cloned.1.call-done, bf16[2048,576]{0,1:T(8,128)(2,1)S(1)} %copy-done), kind=kOutput, calls=%fused_computation.14 | convolution fusion | flops 905969664 | bytes 4816896 | tf_op jit(solution)/shard_map/dot_general | solution.py:34
  136.7 3.5 %all-to-all-start.1 = ((f32[4,96,576]{2,1,0:T(8,128)}), f32[4,96,576]{2,1,0:T(8,128)S(1)}, u32[]{:S(2)}, u32[]{:S(2)}) async-start(f32[4,96,576]{2,1,0:T(8,128)} %bitcast.17), calls=%async_computation.2 | async-start | bytes 1966080 | tf_op jit(solution)/shard_map/all_to_all | solution.py:35
  140.2 0.0 copy-done.6
  140.2 0.6 dynamic-slice.4
  141.5 11.2 %all-to-all-done.1 = f32[4,96,576]{2,1,0:T(8,128)S(1)} async-done(((f32[4,96,576]{2,1,0:T(8,128)}), f32[4,96,576]{2,1,0:T(8,128)S(1)}, u32[]{:S(2)}, u32[]{:S(2)}) %all-to-all-start.1) | async-done | bytes 884768 | tf_op jit(solution)/shard_map/all_to_all | solution.py:35
  152.6 0.0 copy-start.4
  152.6 0.9 copy-done.4
  153.6 0.0 copy-start.3
  153.6 2.8 %copy.13 = f32[96,4,576]{2,1,0:T(4,128)} copy(f32[96,4,576]{2,0,1:T(8,128)} %bitcast.16) | data formatting | bytes 1769472 | tf_op jit(solution)/shard_map/all_to_all | solution.py:35
  156.4 2.7 %all_to_all.35 = f32[96,2304]{1,0:T(8,128)} reshape(f32[96,4,576]{2,1,0:T(4,128)} %copy.13) | data formatting | bytes 1769472 | tf_op jit(solution)/shard_map/all_to_all | solution.py:35
  159.1 32.7 %fusion = f32[16,2304]{1,0:T(8,128)S(1)} fusion(f32[96,2304]{1,0:T(8,128)} %all_to_all.35), kind=kCustom, calls=%all-reduce-scatter | all-reduce-scatter fusion | flops 294913 | bytes 1032704
  191.8 1.9 collective-permute-start
  193.8 2.4 %collective-permute-start.1 = (f32[12,2304]{1,0:T(8,128)S(1)}, f32[12,2304]{1,0:T(8,128)S(1)}, u32[]{:S(2)}, u32[]{:S(2)}) collective-permute-start(f32[12,2304]{1,0:T(8,128)S(1)} %slice), channel_id=1, source_target_pairs={{0,2},{1,3},{2,4},{3,5},{4,6},{5,7},{8,10},{9,11},{10,12},{11,13},... | collective-permute-start | bytes 331784
  196.2 0.0 copy-done.3
  196.2 5.0 %fusion.8 = f32[2048,576]{0,1:T(8,128)} fusion(bf16[384,2048]{1,0:T(8,128)(2,1)} %all-gather.2.cloned.1.call-done, bf16[384,576]{1,0:T(8,128)(2,1)S(1)} %bitcast.15), kind=kOutput, calls=%fused_computation.13 | convolution fusion | flops 905969664 | bytes 6733824 | tf_op jit(solution)/shard_map/dot_general | solution.py:31
  201.2 2.0 collective-permute-done.1
  203.3 0.0 collective-permute-done
  203.3 0.4 concatenate
  203.7 0.7 constant_dynamic-slice_fusion
  (3 shorter events, 0.0 us)
Async XLA Ops:
  7.2 15.5 %copy-start = (bf16[2048,576]{0,1:T(8,128)(2,1)S(1)}, bf16[2048,576]{0,1:T(8,128)(2,1)}, u32[]{:S(2)}) copy-start(bf16[2048,576]{0,1:T(8,128)(2,1)} %param.4) | copy-start | bytes 7077892
  7.2 63.5 %reduce-scatter.4.cloned.1.call-start = ((), (), s32[]{:S(2)}) async-start(), calls=%async_computation.3 | async-start | bytes 3932160 | tf_op jit(solution)/shard_map/reduce_scatter | solution.py:12
  21.8 0.8 copy-start.2
  25.7 1.0 copy-start.5
  25.7 107.2 %all-gather.2.cloned.1.call-start = ((), (), s32[]{:S(2)}) async-start(), calls=%async_computation.4 | async-start | bytes 1966080 | tf_op jit(solution)/shard_map/all_gather | solution.py:30
  70.6 30.4 %copy-start.1 = (f32[96,2048]{1,0:T(8,128)S(1)}, f32[96,2048]{1,0:T(8,128)}, u32[]{:S(2)}) copy-start(f32[96,2048]{1,0:T(8,128)} %reduce-scatter.4.cloned.1.call-done) | copy-start | bytes 2359300
  102.2 38.0 %copy-start.6 = (u32[32]{0:T(128)S(1)}, u32[32]{0:T(128)}, u32[]{:S(2)}) copy-start(u32[32]{0:T(128)} %constant.10) | copy-start | bytes 388
  136.7 15.9 %all-to-all-start.1 = ((f32[4,96,576]{2,1,0:T(8,128)}), f32[4,96,576]{2,1,0:T(8,128)S(1)}, u32[]{:S(2)}, u32[]{:S(2)}) async-start(f32[4,96,576]{2,1,0:T(8,128)} %bitcast.17), calls=%async_computation.2 | async-start | bytes 1966080 | tf_op jit(solution)/shard_map/all_to_all | solution.py:35
  152.6 0.9 copy-start.4
  153.6 42.6 %copy-start.3 = (bf16[96,4,576]{2,0,1:T(8,128)(2,1)S(1)}, bf16[96,4,576]{2,0,1:T(8,128)(2,1)}, u32[]{:S(2)}) copy-start(bf16[96,4,576]{2,0,1:T(8,128)(2,1)} %copy-done.2) | copy-start | bytes 1327108
  191.8 11.4 %collective-permute-start = (f32[16,2304]{1,0:T(8,128)S(1)}, f32[16,2304]{1,0:T(8,128)S(1)}, u32[]{:S(2)}, u32[]{:S(2)}) collective-permute-start(f32[16,2304]{1,0:T(8,128)S(1)} %fusion), channel_id=1, source_target_pairs={{0,1},{1,2},{2,3},{3,4},{4,5},{5,6},{6,7},{8,9},{9,10},{10,11},{11... | collective-permute-start | bytes 442376
  193.8 9.5 %collective-permute-start.1 = (f32[12,2304]{1,0:T(8,128)S(1)}, f32[12,2304]{1,0:T(8,128)S(1)}, u32[]{:S(2)}, u32[]{:S(2)}) collective-permute-start(f32[12,2304]{1,0:T(8,128)S(1)} %slice), channel_id=1, source_target_pairs={{0,2},{1,3},{2,4},{3,5},{4,6},{5,7},{8,10},{9,11},{10,12},{11,13},... | collective-permute-start | bytes 331784
Sparse Core Ops, SparseCore 0:
  25.8 44.7 reduce-scatter.3
  102.3 30.5 all-gather.1
